TPU v7x, 32 devices: a whole 2x2x4 slice. The times are simulated.
32 devices in a mesh: ka: 2 (over x), band: 16 (over z, y, core).
Axes of the slice: x: 2, y: 2, z: 4, core: 2. Of those that a mesh axis runs over, the one named last changes fastest.
Arguments:
- psi_hat: float32 [2, 12, 2, 128, 128, 128], P('ka', None, None, 'band'), may hold values from -1.5 to 1.5
- occupations: int32 [2, 12], P('ka'), may hold values from 0 to 2
- weights: int32 [2], P('ka'), may hold values from 1 to 6
- density_in: float32 [128, 128, 128], P('band'), may hold values from -12 to 12
- dens_hist: float32 [8, 128, 128, 128], P(None, 'band'), may hold values from -3 to 3
- resid_hist: float32 [8, 128, 128, 128], P(None, 'band'), may hold values from -12 to 12
Outputs:
- out_density: float32 [128, 128, 128], P('band')
- mixed_density: float32 [128, 128, 128], P('band')
All inputs are finite; a program needn't handle non-finite values.
Results may differ from a plain program's by a relative error of at most 0.0003.
Values sent between devices are 32-bit elements; how exact they have to be, the bound alone decides.
A program may use at most 128 MiB of HBM per device.

v0:
```python
from functools import partial

import jax
import jax.numpy as jnp
import numpy as np
from jax import lax
from jax.experimental import pallas as pl
from jax.experimental.pallas import tpu as pltpu
from jax.sharding import PartitionSpec as P

highest = lax.Precision.HIGHEST
beta_mix = 0.3
regular = 0.01
CHUNKS = 3


def rotation_tables(size):
    indices = np.arange(size)
    angles = (indices[:, None] * indices[None, :] % size) * (2.0 * np.pi / size)
    cosine, sine = np.cos(angles), np.sin(angles)
    table = np.block([[cosine, sine], [-sine, cosine]]).astype(np.float32)
    high = table.astype(jnp.bfloat16)
    low = (table - high.astype(np.float32)).astype(jnp.bfloat16)
    return high, low


def split(value):
    high = value.astype(jnp.bfloat16)
    return high, (value - high.astype(jnp.float32)).astype(jnp.bfloat16)


def dot3(left, right, contract):
    dims = (contract, ((), ()))
    dot = partial(lax.dot_general, dimension_numbers=dims, preferred_element_type=jnp.float32)
    return dot(left[0], right[0]) + (dot(left[0], right[1]) + dot(left[1], right[0]))


def planes_kernel(psi_ref, wh_ref, wl_ref, th_ref, tl_ref, out_ref):
    devices, _, _, depth, planes, size = out_ref.shape
    for p in range(planes):
        pair = jnp.concatenate([psi_ref[0, 0, 0, p], psi_ref[0, 0, 1, p]], axis=1)
        after_kz = dot3((th_ref[...], tl_ref[...]), split(pair), ((1,), (1,)))
        rows = jnp.concatenate([after_kz[:size], after_kz[size:]], axis=1)
        after_ky = dot3(split(rows), (wh_ref[...], wl_ref[...]), ((1,), (0,)))
        for part in range(2):
            piece = after_ky[:, part * size : (part + 1) * size]
            out_ref[:, 0, part, :, p, :] = piece.reshape(devices, depth, size)


def power_kernel(scale_ref, recv_ref, th_ref, tl_ref, prev_ref, out_ref):
    devices, _, _, depth, planes, size = recv_ref.shape
    band = pl.program_id(0)
    factor = scale_ref[band]

    @pl.when(band == 0)
    def _():
        out_ref[...] = prev_ref[...]

    for z in range(0, depth, 2):
        columns = []
        for near in range(2):
            parts = [recv_ref[:, 0, c, z + near].reshape(devices * planes, size) for c in range(2)]
            columns.append(jnp.concatenate(parts, axis=0))
        field = dot3(
            (th_ref[...], tl_ref[...]), split(jnp.concatenate(columns, axis=1)), ((1,), (0,))
        )
        power = field[:size] * field[:size] + field[size:] * field[size:]
        for near in range(2):
            out_ref[z + near] += factor * power[:, near * size : (near + 1) * size]


def shards(psi_hat, occupations, weights, density_in, dens_hist, resid_hist):
    devices, points = lax.axis_size("band"), lax.axis_size("ka")
    _, bands, _, planes, size, _ = psi_hat.shape
    depth = size // devices
    chunks = CHUNKS if bands % CHUNKS == 0 else 1
    count = bands // chunks
    high, low = rotation_tables(size)
    wh, wl, th, tl = (jnp.asarray(t) for t in (high, low, high.T, low.T))

    weight = weights[0].astype(jnp.float32)
    share = weight / lax.psum(weight, "ka")
    factors = occupations[0].astype(jnp.float32) * (share * jnp.float32(1.0 / size**3))

    flops = 3 * 2 * count * planes * size * (2 * size) ** 2
    bytes_each = count * 2 * planes * size * size * 4
    whole = pl.BlockSpec((2 * size, 2 * size), lambda b: (0, 0))
    tile_spec = pl.BlockSpec((devices, 1, 2, depth, planes, size), lambda b: (0, b, 0, 0, 0, 0))
    slab = pl.BlockSpec((depth, size, size), lambda b: (0, 0, 0))
    limit = 40 * 1024 * 1024

    received = []
    for chunk in range(chunks):
        tiles = pl.pallas_call(
            planes_kernel,
            grid=(count,),
            in_specs=[
                pl.BlockSpec(
                    (1, 1, 2, planes, size, size),
                    lambda b, first=chunk * count: (0, first + b, 0, 0, 0, 0),
                ),
                whole, whole, whole, whole,
            ],
            out_specs=tile_spec,
            out_shape=jax.ShapeDtypeStruct(
                (devices, count, 2, depth, planes, size), jnp.float32
            ),
            compiler_params=pltpu.CompilerParams(vmem_limit_bytes=limit),
            cost_estimate=pl.CostEstimate(
                flops=2 * flops, bytes_accessed=2 * bytes_each, transcendentals=0
            ),
        )(psi_hat, wh, wl, th, tl)
        received.append(lax.all_to_all(tiles, "band", split_axis=0, concat_axis=0, tiled=True))

    gram = jnp.einsum("hzxy,gzxy->hg", resid_hist, resid_hist, precision=highest)
    start = jnp.einsum("hzxy,zxy->h", resid_hist, density_in, precision=highest)
    early = lax.psum(jnp.concatenate([gram, start[:, None]], axis=1), ("ka", "band"))
    early = early * jnp.float32(1.0 / points)
    gram, start = early[:, :-1], early[:, -1]
    system = gram + regular * jnp.diag(jnp.diag(gram))
    chol_factor = jnp.linalg.cholesky(system)

    pool = jnp.zeros((depth, size, size), jnp.float32)
    for chunk in range(chunks):
        pool = pl.pallas_call(
            power_kernel,
            grid=(count,),
            in_specs=[
                pl.BlockSpec(memory_space=pltpu.SMEM), tile_spec, whole, whole, slab,
            ],
            out_specs=slab,
            out_shape=jax.ShapeDtypeStruct((depth, size, size), jnp.float32),
            compiler_params=pltpu.CompilerParams(vmem_limit_bytes=limit),
            cost_estimate=pl.CostEstimate(
                flops=flops, bytes_accessed=bytes_each, transcendentals=0
            ),
        )(factors[chunk * count : (chunk + 1) * count], received[chunk], th, tl, pool)

    if points == 2:
        density = pool + lax.ppermute(pool, "ka", [(0, 1), (1, 0)])
    else:
        density = lax.psum(pool, "ka")
    late = lax.psum(jnp.sum(resid_hist * pool, axis=(1, 2, 3)), ("ka", "band"))
    mix_coefs = jax.scipy.linalg.cho_solve((chol_factor, True), late - start)
    history = dens_hist + beta_mix * resid_hist
    update = jnp.sum(mix_coefs[:, None, None, None] * history, axis=0)
    mixed_density = density_in + beta_mix * (density - density_in) - update
    return (density, mixed_density)


def solution(mesh):
    return jax.shard_map(
        shards,
        mesh=mesh,
        in_specs=(
            P("ka", None, None, "band", None, None),
            P("ka", None),
            P("ka"),
            P("band", None, None),
            P(None, "band", None, None),
            P(None, "band", None, None),
        ),
        out_specs=(P("band", None, None), P("band", None, None)),
        check_vma=False,
    )
```

profile of v0, /device:TPU:0, one launch (start us, length us, event | category | flops | bytes accessed | tf_op | source)
XLA Modules:
  0.0 378.7 jit_solution(14751098548045343650)
XLA Ops:
  0.6 0.0 copy-start.3
  0.6 0.9 copy-done.3
  1.5 0.9 copy-done.5
  2.4 0.9 copy-done.7
  3.3 0.9 copy-done.9
  4.3 15.6 %shard_map.115 = f32[16,4,2,8,8,128]{5,4,3,2,1,0:T(8,128)S(1)} custom-call(f32[1,12,2,8,128,128]{5,4,3,2,1,0:T(8,128)} %psi_ref.5, bf16[256,256]{1,0:T(8,128)(2,1)S(1)} %copy-done.7, bf16[256,256]{1,0:T(8,128)(2,1)S(1)} %copy-done.9, bf16[256,256]{1,0:T(8,128)(2,1)S(1)} %copy-done.3, bf16[256,256]{1,0:T(8,128)(2,1)S(1)} %copy-done.5), custom_call_target="tpu_custom_call" | custom-call | flops 3221225472 | bytes 8388608 | tf_op jit(solution)/shard_map/pallas_call | solution.py:94
  19.8 0.0 copy-start.2
  19.8 2.0 copy-done.2
  21.8 7.6 %all-to-all-start.2 = ((f32[16,4,2,8,8,128]{5,4,3,2,1,0:T(8,128)}), f32[16,4,2,8,8,128]{5,4,3,2,1,0:T(8,128)}, u32[]{:S(2)}, u32[]{:S(2)}) async-start(f32[16,4,2,8,8,128]{5,4,3,2,1,0:T(8,128)} %copy-done.2), calls=%async_computation.2 | async-start | bytes 8388608 | tf_op jit(solution)/shard_map/all_to_all | solution.py:113
  29.4 0.0 copy-done.4
  29.5 15.6 %shard_map.114 = f32[16,4,2,8,8,128]{5,4,3,2,1,0:T(8,128)S(1)} custom-call(f32[1,12,2,8,128,128]{5,4,3,2,1,0:T(8,128)} %psi_ref.5, bf16[256,256]{1,0:T(8,128)(2,1)S(1)} %copy-done.8, bf16[256,256]{1,0:T(8,128)(2,1)S(1)} %copy-done.10, bf16[256,256]{1,0:T(8,128)(2,1)S(1)} %copy-done.4, bf16[256,256]{1,0:T(8,128)(2,1)S(1)} %copy-done.6), custom_call_target="tpu_custom_call" | custom-call | flops 3221225472 | bytes 8388608 | tf_op jit(solution)/shard_map/pallas_call | solution.py:94
  45.1 1.9 copy-done.1
  47.0 60.0 %all-to-all-done.2.recv_ref = f32[16,4,2,8,8,128]{5,4,3,2,1,0:T(8,128)} async-done(((f32[16,4,2,8,8,128]{5,4,3,2,1,0:T(8,128)}), f32[16,4,2,8,8,128]{5,4,3,2,1,0:T(8,128)}, u32[]{:S(2)}, u32[]{:S(2)}) %all-to-all-start.2) | async-done | bytes 4194336 | tf_op jit(solution)/shard_map/all_to_all | solution.py:113
  107.0 19.7 %all-to-all-start.1 = ((f32[16,4,2,8,8,128]{5,4,3,2,1,0:T(8,128)}), f32[16,4,2,8,8,128]{5,4,3,2,1,0:T(8,128)}, u32[]{:S(2)}, u32[]{:S(2)}) async-start(f32[16,4,2,8,8,128]{5,4,3,2,1,0:T(8,128)} %copy-done.1), calls=%async_computation.1 | async-start | bytes 8388608 | tf_op jit(solution)/shard_map/all_to_all | solution.py:113
  126.7 15.6 %shard_map.113 = f32[16,4,2,8,8,128]{5,4,3,2,1,0:T(8,128)S(1)} custom-call(f32[1,12,2,8,128,128]{5,4,3,2,1,0:T(8,128)} %psi_ref.5, bf16[256,256]{1,0:T(8,128)(2,1)S(1)} %copy-done.8, bf16[256,256]{1,0:T(8,128)(2,1)S(1)} %copy-done.10, bf16[256,256]{1,0:T(8,128)(2,1)S(1)} %copy-done.4, bf16[256,256]{1,0:T(8,128)(2,1)S(1)} %copy-done.6), custom_call_target="tpu_custom_call" | custom-call | flops 3221225472 | bytes 8388608 | tf_op jit(solution)/shard_map/pallas_call | solution.py:94
  142.3 2.0 copy-done
  144.2 60.0 %all-to-all-done.1.recv_ref = f32[16,4,2,8,8,128]{5,4,3,2,1,0:T(8,128)} async-done(((f32[16,4,2,8,8,128]{5,4,3,2,1,0:T(8,128)}), f32[16,4,2,8,8,128]{5,4,3,2,1,0:T(8,128)}, u32[]{:S(2)}, u32[]{:S(2)}) %all-to-all-start.1) | async-done | bytes 4194336 | tf_op jit(solution)/shard_map/all_to_all | solution.py:113
  204.2 19.8 %all-to-all-start = ((f32[16,4,2,8,8,128]{5,4,3,2,1,0:T(8,128)}), f32[16,4,2,8,8,128]{5,4,3,2,1,0:T(8,128)}, u32[]{:S(2)}, u32[]{:S(2)}) async-start(f32[16,4,2,8,8,128]{5,4,3,2,1,0:T(8,128)} %copy-done), calls=%async_computation | async-start | bytes 8388608 | tf_op jit(solution)/shard_map/all_to_all | solution.py:113
  224.7 6.3 %psum.21 = f32[]{:T(128)} all-reduce(f32[]{:T(128)} %bitcast), channel_id=1, replica_groups=mesh['ka'=2,'band'=16] {'ka'}, use_global_device_ids=true, to_apply=%region_0.0 | all-reduce | flops 1 | bytes 8 | tf_op jit(solution)/shard_map/psum | solution.py:82
  231.7 0.0 copy-start.11
  231.7 0.0 copy-start.14
  231.7 17.7 %fusion.4 = f32[8,8]{0,1:T(8,128)S(1)} fusion(f32[8,8,128,128]{3,2,1,0:T(8,128)} %param.15), kind=kOutput, calls=%fused_computation.7 | convolution fusion | flops 100663296 | bytes 4194560 | tf_op jit(solution)/shard_map/hzxy,gzxy->hg/dot_general | solution.py:115
  249.4 0.0 copy-done.11
  249.4 10.3 %fusion.7 = f32[8,1]{0,1:T(1,128)S(1)} fusion(f32[8,8,128,128]{3,2,1,0:T(8,128)S(1)} %copy-done.11, f32[8,128,128,1]{2,1,0,3:T(8,128)S(1)} %bitcast.46), kind=kOutput, calls=%fused_computation.8 | convolution fusion | flops 12582912 | bytes 4718624 | tf_op jit(solution)/shard_map/hzxy,zxy->h/dot_general | solution.py:116
  259.7 0.0 copy-done.14
  259.7 0.1 slice_bitcast_fusion.1
  259.8 4.5 %shard_map.116.prev_ref = f32[8,128,128]{2,1,0:T(8,128)S(1)} custom-call(f32[4]{0:T(128)S(1)} %get-tuple-element.6.scale_ref, f32[16,4,2,8,8,128]{5,4,3,2,1,0:T(8,128)} %all-to-all-done.2.recv_ref, bf16[256,256]{1,0:T(8,128)(2,1)S(1)} %copy-done.4, bf16[256,256]{1,0:T(8,128)(2,1)S(1)} %copy-done.6, f32[8,128,128]{2,1,0:T(8,128)S(1)} %broadcast_in_dim.36.prev_ref), custom_call_target="tpu_custom_call" | custom-call | flops 1610612736 | bytes 4194304 | tf_op jit(solution)/shard_map/pallas_call | solution.py:125
  264.3 4.5 %shard_map.117.prev_ref = f32[8,128,128]{2,1,0:T(8,128)S(1)} custom-call(f32[4]{0:T(128)S(1)} %get-tuple-element.7.scale_ref, f32[16,4,2,8,8,128]{5,4,3,2,1,0:T(8,128)} %all-to-all-done.1.recv_ref, bf16[256,256]{1,0:T(8,128)(2,1)S(1)} %copy-done.4, bf16[256,256]{1,0:T(8,128)(2,1)S(1)} %copy-done.6, f32[8,128,128]{2,1,0:T(8,128)S(1)} %shard_map.116.prev_ref), custom_call_target="tpu_custom_call" | custom-call | flops 1610612736 | bytes 4194304 | tf_op jit(solution)/shard_map/pallas_call | solution.py:125
  268.8 32.8 %all-to-all-done.recv_ref = f32[16,4,2,8,8,128]{5,4,3,2,1,0:T(8,128)} async-done(((f32[16,4,2,8,8,128]{5,4,3,2,1,0:T(8,128)}), f32[16,4,2,8,8,128]{5,4,3,2,1,0:T(8,128)}, u32[]{:S(2)}, u32[]{:S(2)}) %all-to-all-start) | async-done | bytes 4194336 | tf_op jit(solution)/shard_map/all_to_all | solution.py:113
  301.6 4.6 %shard_map.118 = f32[8,128,128]{2,1,0:T(8,128)S(1)} custom-call(f32[4]{0:T(128)S(1)} %get-tuple-element.8.scale_ref, f32[16,4,2,8,8,128]{5,4,3,2,1,0:T(8,128)} %all-to-all-done.recv_ref, bf16[256,256]{1,0:T(8,128)(2,1)S(1)} %copy-done.4, bf16[256,256]{1,0:T(8,128)(2,1)S(1)} %copy-done.6, f32[8,128,128]{2,1,0:T(8,128)S(1)} %shard_map.117.prev_ref), custom_call_target="tpu_custom_call" | custom-call | flops 1610612736 | bytes 4194304 | tf_op jit(solution)/shard_map/pallas_call | solution.py:125
  306.2 0.0 copy-done.12
  306.2 0.6 multiply_reduce_fusion.1
  306.8 1.5 collective-permute-start
  308.3 60.8 %all-reduce = (f32[8,9]{0,1:T(8,128)S(1)}, f32[8]{0:T(128)S(1)}) all-reduce(f32[8,9]{0,1:T(8,128)S(1)} %pad_maximum_fusion, f32[8]{0:T(128)S(1)} %multiply_reduce_fusion.1), channel_id=1, replica_groups=mesh['ka'=2,'band'=16] {'ka','band'}, use_global_device_ids=true, to_apply=%region_1.0 | all-reduce | flops 80 | bytes 640 | tf_op jit(solution)/shard_map/psum | solution.py:117
  369.1 0.6 gather_fusion
  369.8 0.1 copy.23
  369.9 0.7 cholesky.16
  370.6 0.1 copy.24
  370.6 0.2 select_reduce_fusion
  370.8 0.6 compare_reduce_fusion
  371.4 0.6 select_select_fusion
  372.1 0.1 copy.26
  372.2 0.6 custom-call.10
  372.8 0.1 convolution_bitcast_fusion.1
  372.9 0.1 convolution_bitcast_fusion
  373.1 4.6 %multiply_reduce_fusion = f32[8,128,128]{2,1,0:T(8,128)S(1)} fusion(f32[8,8,128,128]{3,2,1,0:T(8,128)} %param.14, f32[8,8,128,128]{3,2,1,0:T(8,128)} %param.15, f32[8]{0:T(128)S(1)} %convolution_bitcast_fusion), kind=kLoop, calls=%fused_computation.1 | loop fusion | flops 4063232 | bytes 8912928 | tf_op jit(solution)/shard_map/reduce_sum | solution.py:146
  377.6 0.0 collective-permute-done
  377.6 1.1 add_subtract_fusion
  (23 shorter events, 0.1 us)
Async XLA Ops:
  0.6 0.9 copy-start.3
  1.5 0.9 copy-start.5
  2.4 0.9 copy-start.7
  3.3 0.9 copy-start.9
  19.8 2.0 copy-start.2
  21.8 7.6 %copy-start.4 = (bf16[256,256]{1,0:T(8,128)(2,1)S(1)}, bf16[256,256]{1,0:T(8,128)(2,1)}, u32[]{:S(2)}) copy-start(bf16[256,256]{1,0:T(8,128)(2,1)} %constant.78.clone.th_ref) | copy-start | bytes 393220
  21.8 7.6 %copy-start.6 = (bf16[256,256]{1,0:T(8,128)(2,1)S(1)}, bf16[256,256]{1,0:T(8,128)(2,1)}, u32[]{:S(2)}) copy-start(bf16[256,256]{1,0:T(8,128)(2,1)} %constant.79.clone.tl_ref) | copy-start | bytes 393220
  21.8 7.6 %copy-start.8 = (bf16[256,256]{1,0:T(8,128)(2,1)S(1)}, bf16[256,256]{1,0:T(8,128)(2,1)}, u32[]{:S(2)}) copy-start(bf16[256,256]{1,0:T(8,128)(2,1)} %constant.76.clone.wh_ref) | copy-start | bytes 393220
  21.8 7.7 %copy-start.10 = (bf16[256,256]{1,0:T(8,128)(2,1)S(1)}, bf16[256,256]{1,0:T(8,128)(2,1)}, u32[]{:S(2)}) copy-start(bf16[256,256]{1,0:T(8,128)(2,1)} %constant.77.clone.wl_ref) | copy-start | bytes 393220
  21.8 85.2 %all-to-all-start.2 = ((f32[16,4,2,8,8,128]{5,4,3,2,1,0:T(8,128)}), f32[16,4,2,8,8,128]{5,4,3,2,1,0:T(8,128)}, u32[]{:S(2)}, u32[]{:S(2)}) async-start(f32[16,4,2,8,8,128]{5,4,3,2,1,0:T(8,128)} %copy-done.2), calls=%async_computation.2 | async-start | bytes 8388608 | tf_op jit(solution)/shard_map/all_to_all | solution.py:113
  45.1 1.9 copy-start.1
  107.0 97.2 %all-to-all-start.1 = ((f32[16,4,2,8,8,128]{5,4,3,2,1,0:T(8,128)}), f32[16,4,2,8,8,128]{5,4,3,2,1,0:T(8,128)}, u32[]{:S(2)}, u32[]{:S(2)}) async-start(f32[16,4,2,8,8,128]{5,4,3,2,1,0:T(8,128)} %copy-done.1), calls=%async_computation.1 | async-start | bytes 8388608 | tf_op jit(solution)/shard_map/all_to_all | solution.py:113
  142.3 2.0 copy-start
  204.2 45.1 %copy-start.13 = (f32[8,128,128]{2,1,0:T(8,128)S(1)}, f32[8,128,128]{2,1,0:T(8,128)}, u32[]{:S(2)}) copy-start(f32[8,128,128]{2,1,0:T(8,128)} %param.13) | copy-start | bytes 1572868
  204.2 97.4 %all-to-all-start = ((f32[16,4,2,8,8,128]{5,4,3,2,1,0:T(8,128)}), f32[16,4,2,8,8,128]{5,4,3,2,1,0:T(8,128)}, u32[]{:S(2)}, u32[]{:S(2)}) async-start(f32[16,4,2,8,8,128]{5,4,3,2,1,0:T(8,128)} %copy-done), calls=%async_computation | async-start | bytes 8388608 | tf_op jit(solution)/shard_map/all_to_all | solution.py:113
  231.7 17.7 %copy-start.11 = (f32[8,8,128,128]{3,2,1,0:T(8,128)S(1)}, f32[8,8,128,128]{3,2,1,0:T(8,128)}, u32[]{:S(2)}) copy-start(f32[8,8,128,128]{3,2,1,0:T(8,128)} %param.15) | copy-start | bytes 12582916
  231.7 28.0 %copy-start.14 = (s32[1,12]{1,0:T(1,128)S(1)}, s32[1,12]{1,0:T(1,128)}, u32[]{:S(2)}) copy-start(s32[1,12]{1,0:T(1,128)} %param.11) | copy-start | bytes 148
  301.6 4.6 %copy-start.12 = (f32[8,8,128,128]{3,2,1,0:T(8,128)S(1)}, f32[8,8,128,128]{3,2,1,0:T(8,128)}, u32[]{:S(2)}) copy-start(f32[8,8,128,128]{3,2,1,0:T(8,128)} %param.15) | copy-start | bytes 12582916
  306.8 70.8 %collective-permute-start = (f32[8,128,128]{2,1,0:T(8,128)S(1)}, f32[8,128,128]{2,1,0:T(8,128)S(1)}, u32[]{:S(2)}, u32[]{:S(2)}) collective-permute-start(f32[8,128,128]{2,1,0:T(8,128)S(1)} %shard_map.118), channel_id=1, source_target_pairs={{0,16},{16,0},{1,17},{17,1},{2,18},{18,2},{3,19},{19,3},{4,20},{20... | collective-permute-start | bytes 1572872 | tf_op jit(solution)/shard_map/ppermute | solution.py:140
where the time goes:
time: 379 us
  waiting for transfers between devices  153 us (40%)
  blocking collectives  67.1 us (18%)
  Pallas kernels  60.3 us (16%)
  starting transfers between devices  48.6 us (13%)
  matrix products  28.2 us (7%)
  local copies, waits for them, and re-layouts  10.5 us (3%)
  other arithmetic  9.07 us (2%)
    all_to_all x3, waiting for transfers between devices, shards(): lax.all_to_all(tiles, 'band', split_axis=0, concat_axis=0, tiled=True)  153 us
    psum x1, blocking collectives, shards(): lax.psum(jnp.concatenate([gram, start[:, None]], axis=1), ('ka', 'band'))  60.8 us
    all_to_all x3, starting transfers between devices, shards(): lax.all_to_all(tiles, 'band', split_axis=0, concat_axis=0, tiled=True)  47.1 us
    pallas_call x3, Pallas kernels, shards(): pl.pallas_call(planes_kernel, grid=(count,), in_specs=[pl.BlockSpec((1, 1...  46.7 us
    dot_general x1, matrix products, shards(): jnp.einsum('hzxy,gzxy->hg', resid_hist, resid_hist, precision=highest)  17.7 us
    pallas_call x3, Pallas kernels, shards(): pl.pallas_call(power_kernel, grid=(count,), in_specs=[pl.BlockSpec(memory...  13.6 us
    dot_general x1, matrix products, shards(): start = jnp.einsum('hzxy,zxy->h', resid_hist, density_in, precision=highest)  10.3 us
    unnamed x30, local copies, waits for them, and re-layouts  9.53 us
  transfers between devices with their start and end apart: 4, of which 3 were waited for; matrix products, arithmetic and copies ran while one was open for 10% of the time, Pallas kernels for 11%

commit v1 on v0

v1 whole, which is shorter than its diff:
```python
from functools import partial

import jax
import jax.numpy as jnp
import numpy as np
from jax import lax
from jax.experimental import pallas as pl
from jax.experimental.pallas import tpu as pltpu
from jax.sharding import PartitionSpec as P

beta_mix = 0.3
regular = 0.01
LAG = 3
MESH = pl.DeviceIdType.MESH


def rotation_tables(size):
    indices = np.arange(size)
    angles = (indices[:, None] * indices[None, :] % size) * (2.0 * np.pi / size)
    cosine, sine = np.cos(angles), np.sin(angles)
    table = np.block([[cosine, sine], [-sine, cosine]]).astype(np.float32)
    high = table.astype(jnp.bfloat16)
    low = (table - high.astype(np.float32)).astype(jnp.bfloat16)
    return np.stack([high, low, high.T, low.T])


def split(value):
    high = value.astype(jnp.bfloat16)
    return high, (value - high.astype(jnp.float32)).astype(jnp.bfloat16)


def dot3(left, right, contract):
    dims = (contract, ((), ()))
    dot = partial(lax.dot_general, dimension_numbers=dims, preferred_element_type=jnp.float32)
    return dot(left[0], right[0]) + (dot(left[0], right[1]) + dot(left[1], right[0]))


def partner(index, step, count):
    if count & (count - 1):
        return lax.rem(index + step, count)
    result, bit = index, 1
    while bit < count:
        if step & bit:
            result = result + bit * (1 - 2 * lax.rem(index // bit, 2))
        bit *= 2
    return result


def total(value):
    return jnp.sum(jnp.sum(value, axis=0, keepdims=True), axis=1, keepdims=True)


def step_kernel(
    occ_ref, weight_ref, tables_hbm, psi_hbm, density_in_hbm, dens_hbm, resid_hbm,
    density_hbm, mixed_hbm,
    tables, psi, send, recv, pools, resid, dens, density_in, mixed, share, wbuf, grams, lates,
    late_acc, inverse,
    in_sem, psi_sem, send_sem, recv_sem, small_send, small_recv, pool_send, pool_recv, out_sem,
):
    points, devices = lax.axis_size("ka"), lax.axis_size("band")
    bands, _, depth, _, planes, size = send.shape[0], *send.shape[1:]
    hist = resid.shape[0]
    everyone = points * devices
    pairs = depth // 2
    ka, me = lax.axis_index("ka"), lax.axis_index("band")
    flat = ka * devices + me
    steps = range(devices - 1, 0, -1)
    some_band = (ka, partner(me, 1, devices))
    some_point = (lax.rem(ka + 1, points), me)

    def remote(source, target, send_s, recv_s, device):
        return pltpu.make_async_remote_copy(
            src_ref=source, dst_ref=target, send_sem=send_s, recv_sem=recv_s,
            device_id=device, device_id_type=MESH,
        )

    def psi_copy(band, slot):
        return pltpu.make_async_copy(psi_hbm.at[0, band], psi.at[slot], psi_sem.at[slot])

    tables_copy = pltpu.make_async_copy(tables_hbm, tables, in_sem.at[0])
    resid_copy = pltpu.make_async_copy(resid_hbm, resid, in_sem.at[1])
    dens_copy = pltpu.make_async_copy(dens_hbm, dens, in_sem.at[2])
    base_copy = pltpu.make_async_copy(density_in_hbm, density_in, in_sem.at[3])

    psi_copy(0, 0).start()
    tables_copy.start()
    psi_copy(1, 1).start()
    barrier = pltpu.get_barrier_semaphore()

    def greet(step, carry):
        other = lax.rem(flat + step, everyone)
        pl.semaphore_signal(
            barrier, inc=1, device_id=(other // devices, lax.rem(other, devices)),
            device_id_type=MESH,
        )
        return carry

    lax.fori_loop(1, everyone, greet, 0)
    base_copy.start()
    resid_copy.start()
    dens_copy.start()
    pools[pl.ds(ka, 1)] = jnp.zeros((1, depth, size, size), jnp.float32)
    late_acc[...] = jnp.zeros(late_acc.shape, jnp.float32)
    wbuf[pl.ds(ka, 1)] = jnp.full((1, 1, 128), weight_ref[0].astype(jnp.float32))
    tables_copy.wait()

    def produce(band, slot):
        psi_copy(band, slot).wait()
        for p in range(planes):
            pair = jnp.concatenate([psi[slot, 0, p], psi[slot, 1, p]], axis=1)
            after_kz = dot3((tables[2], tables[3]), split(pair), ((1,), (1,)))
            rows = jnp.concatenate([after_kz[:size], after_kz[size:]], axis=1)
            after_ky = dot3(split(rows), (tables[0], tables[1]), ((1,), (0,)))
            for part in range(2):
                piece = after_ky[:, part * size : (part + 1) * size]
                send[band, :, :, part, p, :] = piece.reshape(devices, depth, size)
        recv[band, pl.ds(me, 1)] = send[band, pl.ds(me, 1)]

    def transform(band, pair):
        columns = []
        for near in range(2):
            z = 2 * pair + near
            parts = [recv[band, :, z, c].reshape(devices * planes, size) for c in range(2)]
            columns.append(jnp.concatenate(parts, axis=0))
        field = dot3(
            (tables[2], tables[3]), split(jnp.concatenate(columns, axis=1)), ((1,), (0,))
        )
        power = field[:size] * field[:size] + field[size:] * field[size:]
        scale = share[...] * occ_ref[0, band].astype(jnp.float32)
        for near in range(2):
            pools[ka, 2 * pair + near] += scale * power[:, near * size : (near + 1) * size]

    def consume(band):
        remote(
            send.at[band, pl.ds(0, devices - 1)], recv.at[band, pl.ds(0, devices - 1)],
            send_sem.at[band], recv_sem.at[band], some_band,
        ).wait_recv()

        def body(pair, carry):
            transform(band, pair)
            return carry

        lax.fori_loop(0, pairs, body, 0)

    def send_weight():
        for step in range(1, points):
            remote(
                wbuf.at[ka], wbuf.at[ka], small_send.at[0], small_recv.at[0],
                (lax.rem(ka + step, points), me),
            ).start()

    def history():
        remote(
            wbuf.at[pl.ds(0, points - 1)], wbuf.at[pl.ds(0, points - 1)],
            small_send.at[0], small_recv.at[0], some_point,
        ).wait()
        weight_total = wbuf[0]
        for k in range(1, points):
            weight_total = weight_total + wbuf[k]
        share[...] = wbuf[ka] / weight_total * jnp.float32(1.0 / size**3)
        base_copy.wait()
        resid_copy.wait()
        dens_copy.wait()
        which = [(h, g) for h in range(hist) for g in range(h + 1)]
        blocks = size // 8

        def body(i, sums):
            z, x = i // blocks, pl.multiple_of(lax.rem(i, blocks) * 8, 8)
            rows = [resid[h, z, pl.ds(x, 8)] for h in range(hist)]
            start = density_in[z, pl.ds(x, 8)]
            for h in range(hist):
                dens[h, z, pl.ds(x, 8)] = dens[h, z, pl.ds(x, 8)] + beta_mix * rows[h]
            products = [rows[h] * rows[g] for h, g in which] + [row * start for row in rows]
            return tuple(s + p for s, p in zip(sums, products))

        zeros = tuple(jnp.zeros((8, size), jnp.float32) for _ in range(len(which) + hist))
        sums = lax.fori_loop(0, depth * blocks, body, zeros)
        lane = lax.broadcasted_iota(jnp.int32, (1, 128), 1)
        row = jnp.zeros((1, 128), jnp.float32)
        for (h, g), value in zip(which, sums):
            here = (lane == h * hist + g) | (lane == g * hist + h)
            row = jnp.where(here, total(value), row)
        for h in range(hist):
            row = jnp.where(lane == hist * hist + h, total(sums[len(which) + h]), row)
        grams[pl.ds(me, 1)] = row[None]
        for step in steps:
            remote(
                grams.at[me], grams.at[me], small_send.at[1], small_recv.at[1],
                (ka, partner(me, step, devices)),
            ).start()

    def factor():
        rest = pl.ds(0, devices - 1)
        remote(
            grams.at[rest], grams.at[rest], small_send.at[1], small_recv.at[1], some_band
        ).wait()
        row = grams[0]
        for d in range(1, devices):
            row = row + grams[d]
        lane = lax.broadcasted_iota(jnp.int32, (hist, 128), 1)
        level = lax.broadcasted_iota(jnp.int32, (hist, 128), 0)
        wide = jnp.broadcast_to(row, (hist, 128))
        start = jnp.zeros((1, 1), jnp.float32)
        gram = jnp.zeros((hist, 128), jnp.float32)
        for g in range(hist):
            picked = jnp.sum(
                jnp.where(lane == level * hist + g, wide, 0.0), axis=1, keepdims=True
            )
            gram = jnp.where(lane == g, picked, gram)
        first = jnp.sum(
            jnp.where(lane == hist * hist + level, wide, 0.0), axis=1, keepdims=True
        )
        start = jnp.sum(jnp.where(lane == level, first, 0.0), axis=0, keepdims=True)
        work = jnp.where(lane == level, gram + regular * gram, gram)
        right = jnp.where(lane == level, jnp.float32(1.0), 0.0)
        for j in range(hist):
            pivot = jnp.sum(
                jnp.where((lane == j) & (level == j), work, 0.0), axis=(0, 1), keepdims=True
            )
            root = jnp.sqrt(pivot)
            column = jnp.sum(jnp.where(lane == j, work, 0.0), axis=1, keepdims=True) / root
            line = jnp.sum(jnp.where(level == j, work, 0.0), axis=0, keepdims=True) / root
            solved = jnp.sum(jnp.where(level == j, right, 0.0), axis=0, keepdims=True) / root
            work = work - column * line
            right = jnp.where(
                level == j, solved, jnp.where(level > j, right - column * solved, right)
            )
        inverse[0:hist] = right
        inverse[hist : hist + 1] = start

    def step(band, carry):
        slot = lax.rem(band, 2)
        produce(band, slot)

        @pl.when(band == 0)
        def _():
            pl.semaphore_wait(barrier, everyone - 1)
            send_weight()

        @pl.when(band < bands - 1)
        def _():
            for s in steps:
                other = partner(me, s, devices)
                remote(
                    send.at[band, other], recv.at[band, me],
                    send_sem.at[band], recv_sem.at[band], (ka, other),
                ).start()

        @pl.when(band == bands - 1)
        def _():
            for pair in range(pairs):
                for s in steps:
                    other = partner(me, s, devices)
                    cut = pl.ds(2 * pair, 2)
                    remote(
                        send.at[bands - 1, other, cut], recv.at[bands - 1, me, cut],
                        send_sem.at[bands - 1 + pair], recv_sem.at[bands - 1 + pair],
                        (ka, other),
                    ).start()

        @pl.when(band + 2 < bands)
        def _():
            psi_copy(band + 2, slot).start()

        @pl.when(band == LAG - 1)
        def _():
            history()

        @pl.when(band >= LAG)
        def _():
            consume(band - LAG)

        return carry

    lax.fori_loop(0, bands, step, 0)
    factor()

    def drain(band, carry):
        consume(band)
        return carry

    lax.fori_loop(bands - LAG, bands - 1, drain, 0)

    def pool_copy(pair, device):
        cut = pl.ds(2 * pair, 2)
        return remote(
            pools.at[ka, cut], pools.at[ka, cut], pool_send.at[pair], pool_recv.at[pair], device
        )

    def pool_wait(pair):
        rest = pools.at[pl.ds(0, points - 1), pl.ds(2 * pair, 2)]
        return remote(rest, rest, pool_send.at[pair], pool_recv.at[pair], some_point)

    def density_out(pair):
        cut = pl.ds(2 * pair, 2)
        return pltpu.make_async_copy(
            mixed.at[0, cut], density_hbm.at[cut], out_sem.at[pair]
        )

    def mixed_out(pair):
        cut = pl.ds(2 * pair, 2)
        return pltpu.make_async_copy(
            mixed.at[1, cut], mixed_hbm.at[cut], out_sem.at[pairs + pair]
        )

    def gather(pair):
        pool_wait(pair).wait()
        for z in (2 * pair, 2 * pair + 1):
            density = pools[0, z]
            for k in range(1, points):
                density = density + pools[k, z]
            start = density_in[z]
            mixed[0, z] = density
            mixed[1, z] = start + beta_mix * (density - start)
        density_out(pair).start()

    for pair in range(pairs):
        cut = pl.ds(2 * pair, 2)
        rest = pl.ds(0, devices - 1)
        remote(
            send.at[bands - 1, rest, cut], recv.at[bands - 1, rest, cut],
            send_sem.at[bands - 1 + pair], recv_sem.at[bands - 1 + pair], some_band,
        ).wait_recv()
        transform(bands - 1, pair)
        for s in range(1, points):
            pool_copy(pair, (lax.rem(ka + s, points), me)).start()
        for h in range(hist):
            value = late_acc[h]
            for z in (2 * pair, 2 * pair + 1):
                product = resid[h, z] * pools[ka, z]
                value = value + jnp.sum(product.reshape(size // 8, 8, size), axis=0)
            late_acc[h] = value
        if pair:
            gather(pair - 1)

    lane = lax.broadcasted_iota(jnp.int32, (hist, 128), 1)
    level = lax.broadcasted_iota(jnp.int32, (hist, 128), 0)
    sums = jnp.sum(jnp.sum(late_acc[...], axis=1), axis=1, keepdims=True)
    row = jnp.sum(jnp.where(lane == level, sums, 0.0), axis=0, keepdims=True)
    lates[pl.ds(flat, 1)] = row[None]

    def tell(step, carry):
        other = lax.rem(flat + step, everyone)
        remote(
            lates.at[flat], lates.at[flat], small_send.at[2], small_recv.at[2],
            (other // devices, lax.rem(other, devices)),
        ).start()
        return carry

    lax.fori_loop(1, everyone, tell, 0)
    gather(pairs - 1)
    rest = lates.at[pl.ds(0, everyone - 1)]
    remote(rest, rest, small_send.at[2], small_recv.at[2], some_band).wait()
    late = lates[0]
    for d in range(1, everyone):
        late = late + lates[d]
    factor_inverse = inverse[0:hist]
    halfway = jnp.sum(
        factor_inverse * (late - inverse[hist : hist + 1]), axis=1, keepdims=True
    )
    coefs = jnp.sum(factor_inverse * halfway, axis=0, keepdims=True)
    coefs = [
        jnp.sum(jnp.where(lane[:1] == h, coefs, 0.0), axis=1, keepdims=True) for h in range(hist)
    ]
    for pair in range(pairs):
        for z in (2 * pair, 2 * pair + 1):
            update = coefs[0] * dens[0, z]
            for h in range(1, hist):
                update = update + coefs[h] * dens[h, z]
            mixed[1, z] = mixed[1, z] - update
        mixed_out(pair).start()

    rest = pl.ds(0, devices - 1)

    def sent(band, carry):
        remote(
            send.at[band, rest], recv.at[band, rest], send_sem.at[band], recv_sem.at[band],
            some_band,
        ).wait_send()
        return carry

    lax.fori_loop(0, bands - 1, sent, 0)
    for pair in range(pairs):
        cut = pl.ds(2 * pair, 2)
        remote(
            send.at[bands - 1, rest, cut], recv.at[bands - 1, rest, cut],
            send_sem.at[bands - 1 + pair], recv_sem.at[bands - 1 + pair], some_band,
        ).wait_send()
        density_out(pair).wait()
        mixed_out(pair).wait()


def shards(psi_hat, occupations, weights, density_in, dens_hist, resid_hist):
    devices, points = lax.axis_size("band"), lax.axis_size("ka")
    _, bands, _, planes, size, _ = psi_hat.shape
    hist = resid_hist.shape[0]
    depth = size // devices
    pairs = depth // 2
    tables = jnp.asarray(rotation_tables(size))
    anywhere = pl.BlockSpec(memory_space=pl.ANY)
    scalars = pl.BlockSpec(memory_space=pltpu.SMEM)
    slab = jax.ShapeDtypeStruct((depth, size, size), jnp.float32)
    f32 = jnp.float32
    dma = pltpu.SemaphoreType.DMA
    return pl.pallas_call(
        step_kernel,
        in_specs=[scalars, scalars] + [anywhere] * 5,
        out_specs=[anywhere, anywhere],
        out_shape=(slab, slab),
        scratch_shapes=[
            pltpu.VMEM(tables.shape, jnp.bfloat16),
            pltpu.VMEM((2, 2, planes, size, size), f32),
            pltpu.VMEM((bands, devices, depth, 2, planes, size), f32),
            pltpu.VMEM((bands, devices, depth, 2, planes, size), f32),
            pltpu.VMEM((points, depth, size, size), f32),
            pltpu.VMEM((hist, depth, size, size), f32),
            pltpu.VMEM((hist, depth, size, size), f32),
            pltpu.VMEM((depth, size, size), f32),
            pltpu.VMEM((2, depth, size, size), f32),
            pltpu.VMEM((1, 128), f32),
            pltpu.VMEM((points, 1, 128), f32),
            pltpu.VMEM((devices, 1, 128), f32),
            pltpu.VMEM((points * devices, 1, 128), f32),
            pltpu.VMEM((hist, 8, size), f32),
            pltpu.VMEM((hist + 8, 128), f32),
            dma((4,)), dma((2,)),
            dma((bands - 1 + pairs,)), dma((bands - 1 + pairs,)),
            dma((3,)), dma((3,)), dma((pairs,)), dma((pairs,)), dma((2 * pairs,)),
        ],
        compiler_params=pltpu.CompilerParams(
            collective_id=0, has_side_effects=True, vmem_limit_bytes=56 * 1024 * 1024
        ),
    )(occupations, weights, tables, psi_hat, density_in, dens_hist, resid_hist)


def solution(mesh):
    return jax.shard_map(
        shards,
        mesh=mesh,
        in_specs=(
            P("ka", None, None, "band", None, None),
            P("ka", None),
            P("ka"),
            P("band", None, None),
            P(None, "band", None, None),
            P(None, "band", None, None),
        ),
        out_specs=(P("band", None, None), P("band", None, None)),
        check_vma=False,
    )
```

time: 379 us -> 296 us (0.78)
  Pallas kernels: 60.3 us -> 291 us
  waiting for transfers between devices: 153 us -> 0 us
  blocking collectives: 67.1 us -> 0 us
  starting transfers between devices: 48.6 us -> 0 us
  matrix products: 28.2 us -> 0 us
  other arithmetic: 9.07 us -> 0 us
  local copies, waits for them, and re-layouts: 10.5 us -> 3.74 us
    pallas_call x6 -> x1, Pallas kernels: 60.3 us -> 291 us  [shards(): pl.pallas_call(step_kernel, in_specs=[scalars, scalars] + [anywhere] * 5,...]
    all_to_all x3 -> x0, waiting for transfers between devices: 153 us -> none  [shards(): lax.all_to_all(tiles, 'band', split_axis=0, concat_axis=0, tiled=True)]
    psum x2 -> x0, blocking collectives: 67.1 us -> none  [the longest x1 60.8 us: shards(): lax.psum(jnp.concatenate([gram, start[:, None]], axis=1), ('ka', 'band'))]
    all_to_all x3 -> x0, starting transfers between devices: 47.1 us -> none  [shards(): lax.all_to_all(tiles, 'band', split_axis=0, concat_axis=0, tiled=True)]
    dot_general x2 -> x0, matrix products: 28 us -> none  [the longest x1 17.7 us: shards(): jnp.einsum('hzxy,gzxy->hg', resid_hist, resid_hist, precision=highest)]
    unnamed x30 -> x2, local copies, waits for them, and re-layouts: 9.53 us -> 3.74 us
    reduce_sum x2 -> x0, other arithmetic: 5.14 us -> none  [the longest x1 4.56 us: shards(): update = jnp.sum(mix_coefs[:, None, None, None] * history, axis=0)]
  transfers between devices with their start and end apart: 4 -> 0, of which waited for: 3 -> 0; matrix products, arithmetic and copies ran while one was open for 10% -> 0% of each run, Pallas kernels for 11% -> 0%
where the time goes in v1:
time: 296 us
  Pallas kernels  291 us (98%)
  local copies, waits for them, and re-layouts  3.74 us (1%)
    pallas_call x1, Pallas kernels, shards(): pl.pallas_call(step_kernel, in_specs=[scalars, scalars] + [anywhere] * 5,...  291 us

profile of v1, /device:TPU:0, one launch (start us, length us, event | category | flops | bytes accessed | tf_op | source)
XLA Modules:
  0.0 296.0 jit_solution(16050077011550750944)
XLA Ops:
  1.3 290.9 %shard_map.86 = (f32[8,128,128]{2,1,0:T(8,128)}, f32[8,128,128]{2,1,0:T(8,128)}) custom-call(s32[1,12]{1,0:T(1,128)} %occ_ref.1, s32[1]{0:T(128)S(6)} %copy.11.weight_ref, bf16[4,256,256]{2,1,0:T(8,128)(2,1)} %constant.2.clone.tables_hbm, f32[1,12,2,8,128,128]{5,4,3,2,1,0:T(8,128)} %psi_hbm.1, f32[8,128,128]{2,1,0:T(8,128)} %density_in_hbm.1, ...), custom_call_target="tpu_custom_call" | custom-call | tf_op jit(solution)/shard_map/pallas_call | solution.py:405
  292.2 1.9 copy.12
  294.1 1.9 copy.13

commit v2 on v1

--- a/solution.py
+++ b/solution.py
@@ -11,6 +11,7 @@
 beta_mix = 0.3
 regular = 0.01
 LAG = 3
+LAST = 2
 MESH = pl.DeviceIdType.MESH
 
 
@@ -51,20 +52,21 @@
 
 
 def step_kernel(
-    occ_ref, weight_ref, tables_hbm, psi_hbm, density_in_hbm, dens_hbm, resid_hbm,
-    density_hbm, mixed_hbm,
-    tables, psi, send, recv, pools, resid, dens, density_in, mixed, share, wbuf, grams, lates,
+    scalar_ref, tables_hbm, psi_hbm, density_in_hbm, dens_hbm, resid_hbm,
+    first_ref, others_ref, update_ref,
+    tables, psi, send, recv, pools, resid, dens, density_in, share, wbuf, grams, lates,
     late_acc, inverse,
-    in_sem, psi_sem, send_sem, recv_sem, small_send, small_recv, pool_send, pool_recv, out_sem,
+    in_sem, psi_sem, send_sem, recv_sem, small_send, small_recv, pool_send, pool_recv,
 ):
     points, devices = lax.axis_size("ka"), lax.axis_size("band")
     bands, _, depth, _, planes, size = send.shape[0], *send.shape[1:]
     hist = resid.shape[0]
     everyone = points * devices
-    pairs = depth // 2
+    pairs, early = depth // 2, bands - LAST
     ka, me = lax.axis_index("ka"), lax.axis_index("band")
     flat = ka * devices + me
-    steps = range(devices - 1, 0, -1)
+    half = devices // 2
+    steps = [s for low in range(half - 1, -1, -1) for s in (half + low, low) if s]
     some_band = (ka, partner(me, 1, devices))
     some_point = (lax.rem(ka + 1, points), me)
 
@@ -101,8 +103,16 @@
     dens_copy.start()
     pools[pl.ds(ka, 1)] = jnp.zeros((1, depth, size, size), jnp.float32)
     late_acc[...] = jnp.zeros(late_acc.shape, jnp.float32)
-    wbuf[pl.ds(ka, 1)] = jnp.full((1, 1, 128), weight_ref[0].astype(jnp.float32))
+    wbuf[pl.ds(ka, 1)] = jnp.full((1, 1, 128), scalar_ref[0, bands])
     tables_copy.wait()
+
+    def send_planes(cut):
+        for s in steps:
+            other = partner(me, s, devices)
+            remote(
+                send.at[0, other, :, :, cut], recv.at[0, me, :, :, cut],
+                send_sem.at[0], recv_sem.at[0], (ka, other),
+            ).start()
 
     def produce(band, slot):
         psi_copy(band, slot).wait()
@@ -114,21 +124,27 @@
             for part in range(2):
                 piece = after_ky[:, part * size : (part + 1) * size]
                 send[band, :, :, part, p, :] = piece.reshape(devices, depth, size)
+            if p == planes // 2 - 1:
+
+                @pl.when(band == 0)
+                def _():
+                    pl.semaphore_wait(barrier, everyone - 1)
+                    send_planes(pl.ds(0, planes // 2))
+
         recv[band, pl.ds(me, 1)] = send[band, pl.ds(me, 1)]
 
-    def transform(band, pair):
+    def transform(band, layers):
         columns = []
-        for near in range(2):
-            z = 2 * pair + near
+        for z in layers:
             parts = [recv[band, :, z, c].reshape(devices * planes, size) for c in range(2)]
             columns.append(jnp.concatenate(parts, axis=0))
         field = dot3(
             (tables[2], tables[3]), split(jnp.concatenate(columns, axis=1)), ((1,), (0,))
         )
         power = field[:size] * field[:size] + field[size:] * field[size:]
-        scale = share[...] * occ_ref[0, band].astype(jnp.float32)
-        for near in range(2):
-            pools[ka, 2 * pair + near] += scale * power[:, near * size : (near + 1) * size]
+        scale = share[...] * scalar_ref[0, band]
+        for i, z in enumerate(layers):
+            pools[ka, z] += scale * power[:, i * size : (i + 1) * size]
 
     def consume(band):
         remote(
@@ -137,7 +153,7 @@
         ).wait_recv()
 
         def body(pair, carry):
-            transform(band, pair)
+            transform(band, (2 * pair, 2 * pair + 1))
             return carry
 
         lax.fori_loop(0, pairs, body, 0)
@@ -234,10 +250,10 @@
 
         @pl.when(band == 0)
         def _():
-            pl.semaphore_wait(barrier, everyone - 1)
+            send_planes(pl.ds(planes // 2, planes // 2))
             send_weight()
 
-        @pl.when(band < bands - 1)
+        @pl.when((band > 0) & (band < early))
         def _():
             for s in steps:
                 other = partner(me, s, devices)
@@ -248,15 +264,17 @@
 
         @pl.when(band == bands - 1)
         def _():
-            for pair in range(pairs):
+            def layer(z, carry):
                 for s in steps:
                     other = partner(me, s, devices)
-                    cut = pl.ds(2 * pair, 2)
+                    tail = pl.ds(early, LAST)
                     remote(
-                        send.at[bands - 1, other, cut], recv.at[bands - 1, me, cut],
-                        send_sem.at[bands - 1 + pair], recv_sem.at[bands - 1 + pair],
-                        (ka, other),
+                        send.at[tail, other, z], recv.at[tail, me, z],
+                        send_sem.at[early + z], recv_sem.at[early + z], (ka, other),
                     ).start()
+                return carry
+
+            lax.fori_loop(0, depth, layer, 0)
 
         @pl.when(band + 2 < bands)
         def _():
@@ -279,60 +297,55 @@
         consume(band)
         return carry
 
-    lax.fori_loop(bands - LAG, bands - 1, drain, 0)
-
-    def pool_copy(pair, device):
-        cut = pl.ds(2 * pair, 2)
+    lax.fori_loop(bands - LAG, early, drain, 0)
+
+    def send_pool(z):
+        for s in range(1, points):
+            remote(
+                pools.at[ka, z], pools.at[ka, z], pool_send.at[z], pool_recv.at[z],
+                (lax.rem(ka + s, points), me),
+            ).start()
+
+    def gather(z):
+        rest = pools.at[pl.ds(0, points - 1), z]
+        remote(rest, rest, pool_send.at[z], pool_recv.at[z], some_point).wait()
+        others = pools[1, z]
+        for k in range(2, points):
+            others = others + pools[k, z]
+        first_ref[z] = pools[0, z]
+        others_ref[z] = others
+
+    def last_bands(z):
         return remote(
-            pools.at[ka, cut], pools.at[ka, cut], pool_send.at[pair], pool_recv.at[pair], device
+            send.at[pl.ds(early, LAST), pl.ds(0, devices - 1), z],
+            recv.at[pl.ds(early, LAST), pl.ds(0, devices - 1), z],
+            send_sem.at[early + z], recv_sem.at[early + z], some_band,
         )
 
-    def pool_wait(pair):
-        rest = pools.at[pl.ds(0, points - 1), pl.ds(2 * pair, 2)]
-        return remote(rest, rest, pool_send.at[pair], pool_recv.at[pair], some_point)
-
-    def density_out(pair):
-        cut = pl.ds(2 * pair, 2)
-        return pltpu.make_async_copy(
-            mixed.at[0, cut], density_hbm.at[cut], out_sem.at[pair]
-        )
-
-    def mixed_out(pair):
-        cut = pl.ds(2 * pair, 2)
-        return pltpu.make_async_copy(
-            mixed.at[1, cut], mixed_hbm.at[cut], out_sem.at[pairs + pair]
-        )
-
-    def gather(pair):
-        pool_wait(pair).wait()
-        for z in (2 * pair, 2 * pair + 1):
-            density = pools[0, z]
-            for k in range(1, points):
-                density = density + pools[k, z]
-            start = density_in[z]
-            mixed[0, z] = density
-            mixed[1, z] = start + beta_mix * (density - start)
-        density_out(pair).start()
-
-    for pair in range(pairs):
-        cut = pl.ds(2 * pair, 2)
-        rest = pl.ds(0, devices - 1)
-        remote(
-            send.at[bands - 1, rest, cut], recv.at[bands - 1, rest, cut],
-            send_sem.at[bands - 1 + pair], recv_sem.at[bands - 1 + pair], some_band,
-        ).wait_recv()
-        transform(bands - 1, pair)
-        for s in range(1, points):
-            pool_copy(pair, (lax.rem(ka + s, points), me)).start()
+    def finish(z):
+        last_bands(z).wait_recv()
+        for band in range(early, bands):
+            transform(band, (z,))
+
+    def project(z):
         for h in range(hist):
-            value = late_acc[h]
-            for z in (2 * pair, 2 * pair + 1):
-                product = resid[h, z] * pools[ka, z]
-                value = value + jnp.sum(product.reshape(size // 8, 8, size), axis=0)
-            late_acc[h] = value
-        if pair:
-            gather(pair - 1)
-
+            product = resid[h, z] * pools[ka, z]
+            late_acc[h] += jnp.sum(product.reshape(size // 8, 8, size), axis=0)
+
+    def layer(z, carry):
+        finish(z)
+        project(z)
+        send_pool(z)
+
+        @pl.when(z > 0)
+        def _():
+            gather(z - 1)
+
+        return carry
+
+    lax.fori_loop(0, depth - 1, layer, 0)
+    finish(depth - 1)
+    project(depth - 1)
     lane = lax.broadcasted_iota(jnp.int32, (hist, 128), 1)
     level = lax.broadcasted_iota(jnp.int32, (hist, 128), 0)
     sums = jnp.sum(jnp.sum(late_acc[...], axis=1), axis=1, keepdims=True)
@@ -348,7 +361,10 @@
         return carry
 
     lax.fori_loop(1, everyone, tell, 0)
-    gather(pairs - 1)
+    send_pool(depth - 1)
+    if depth > 1:
+        gather(depth - 2)
+    gather(depth - 1)
     rest = lates.at[pl.ds(0, everyone - 1)]
     remote(rest, rest, small_send.at[2], small_recv.at[2], some_band).wait()
     late = lates[0]
@@ -362,13 +378,11 @@
     coefs = [
         jnp.sum(jnp.where(lane[:1] == h, coefs, 0.0), axis=1, keepdims=True) for h in range(hist)
     ]
-    for pair in range(pairs):
-        for z in (2 * pair, 2 * pair + 1):
-            update = coefs[0] * dens[0, z]
-            for h in range(1, hist):
-                update = update + coefs[h] * dens[h, z]
-            mixed[1, z] = mixed[1, z] - update
-        mixed_out(pair).start()
+    for z in range(depth):
+        update = coefs[0] * dens[0, z]
+        for h in range(1, hist):
+            update = update + coefs[h] * dens[h, z]
+        update_ref[z] = update
 
     rest = pl.ds(0, devices - 1)
 
@@ -379,15 +393,13 @@
         ).wait_send()
         return carry
 
-    lax.fori_loop(0, bands - 1, sent, 0)
-    for pair in range(pairs):
-        cut = pl.ds(2 * pair, 2)
-        remote(
-            send.at[bands - 1, rest, cut], recv.at[bands - 1, rest, cut],
-            send_sem.at[bands - 1 + pair], recv_sem.at[bands - 1 + pair], some_band,
-        ).wait_send()
-        density_out(pair).wait()
-        mixed_out(pair).wait()
+    lax.fori_loop(0, early, sent, 0)
+
+    def last_sent(z, carry):
+        last_bands(z).wait_send()
+        return carry
+
+    lax.fori_loop(0, depth, last_sent, 0)
 
 
 def shards(psi_hat, occupations, weights, density_in, dens_hist, resid_hist):
@@ -395,18 +407,19 @@
     _, bands, _, planes, size, _ = psi_hat.shape
     hist = resid_hist.shape[0]
     depth = size // devices
-    pairs = depth // 2
     tables = jnp.asarray(rotation_tables(size))
-    anywhere = pl.BlockSpec(memory_space=pl.ANY)
+    anywhere = pl.BlockSpec(memory_space=pltpu.HBM)
     scalars = pl.BlockSpec(memory_space=pltpu.SMEM)
+    numbers = jnp.concatenate([occupations[0], weights]).astype(jnp.float32)[None]
+    resident = pl.BlockSpec(memory_space=pltpu.VMEM)
     slab = jax.ShapeDtypeStruct((depth, size, size), jnp.float32)
     f32 = jnp.float32
     dma = pltpu.SemaphoreType.DMA
-    return pl.pallas_call(
+    first, others, update = pl.pallas_call(
         step_kernel,
-        in_specs=[scalars, scalars] + [anywhere] * 5,
-        out_specs=[anywhere, anywhere],
-        out_shape=(slab, slab),
+        in_specs=[scalars] + [anywhere] * 5,
+        out_specs=[resident] * 3,
+        out_shape=(slab, slab, slab),
         scratch_shapes=[
             pltpu.VMEM(tables.shape, jnp.bfloat16),
             pltpu.VMEM((2, 2, planes, size, size), f32),
@@ -416,7 +429,6 @@
             pltpu.VMEM((hist, depth, size, size), f32),
             pltpu.VMEM((hist, depth, size, size), f32),
             pltpu.VMEM((depth, size, size), f32),
-            pltpu.VMEM((2, depth, size, size), f32),
             pltpu.VMEM((1, 128), f32),
             pltpu.VMEM((points, 1, 128), f32),
             pltpu.VMEM((devices, 1, 128), f32),
@@ -424,13 +436,15 @@
             pltpu.VMEM((hist, 8, size), f32),
             pltpu.VMEM((hist + 8, 128), f32),
             dma((4,)), dma((2,)),
-            dma((bands - 1 + pairs,)), dma((bands - 1 + pairs,)),
-            dma((3,)), dma((3,)), dma((pairs,)), dma((pairs,)), dma((2 * pairs,)),
+            dma((bands - LAST + depth,)), dma((bands - LAST + depth,)),
+            dma((3,)), dma((3,)), dma((depth,)), dma((depth,)),
         ],
         compiler_params=pltpu.CompilerParams(
-            collective_id=0, has_side_effects=True, vmem_limit_bytes=56 * 1024 * 1024
+            collective_id=0, has_side_effects=True, vmem_limit_bytes=52 * 1024 * 1024
         ),
-    )(occupations, weights, tables, psi_hat, density_in, dens_hist, resid_hist)
+    )(numbers, tables, psi_hat, density_in, dens_hist, resid_hist)
+    density = first + others
+    return density, density_in + beta_mix * (density - density_in) - update
 
 
 def solution(mesh):

time: 296 us -> 289 us (0.976)
  Pallas kernels: 291 us -> 286 us
  local copies, waits for them, and re-layouts: 3.74 us -> 0.01 us
    pallas_call x1, Pallas kernels: 291 us -> 286 us  [shards(): pl.pallas_call(step_kernel, in_specs=[scalars] + [anywhere] * 5, out_spec...]
    unnamed x2, local copies, waits for them, and re-layouts: 3.74 us -> 0.01 us
where the time goes in v2:
time: 289 us
  Pallas kernels  286 us (99%)
    pallas_call x1, Pallas kernels, shards(): pl.pallas_call(step_kernel, in_specs=[scalars] + [anywhere] * 5, out_spec...  286 us

profile of v2, /device:TPU:0, one launch (start us, length us, event | category | flops | bytes accessed | tf_op | source)
XLA Modules:
  0.0 289.1 jit_solution(6085723831402312038)
XLA Ops:
  1.3 0.7 add_convert_fusion.scalar_ref
  2.0 0.0 copy-start
  2.0 286.0 %shard_map.86 = (f32[8,128,128]{2,1,0:T(8,128)S(1)}, f32[8,128,128]{2,1,0:T(8,128)S(1)}, f32[8,128,128]{2,1,0:T(8,128)S(1)}) custom-call(f32[1,13]{1,0:T(1,128)S(1)} %add_convert_fusion.scalar_ref, bf16[4,256,256]{2,1,0:T(8,128)(2,1)} %constant.4.clone.tables_hbm, f32[1,12,2,8,128,128]{5,4,3,2,1,0:T(8,128)} %psi_hbm.1, f32[8,128,128]{2,1,0:T(8,128)} %density_in_hbm.1, ...), custom_call_target="tpu_custom_call" | custom-call | tf_op jit(solution)/shard_map/pallas_call | solution.py:418
  288.0 0.0 copy-done
  288.1 1.1 add_subtract_fusion
Async XLA Ops:
  2.0 286.0 %copy-start = (f32[8,128,128]{2,1,0:T(8,128)S(1)}, f32[8,128,128]{2,1,0:T(8,128)}, u32[]{:S(2)}) copy-start(f32[8,128,128]{2,1,0:T(8,128)} %density_in_hbm.1) | copy-start | bytes 1572868

commit v3 on v2

--- a/solution.py
+++ b/solution.py
@@ -11,7 +11,7 @@
 beta_mix = 0.3
 regular = 0.01
 LAG = 3
-LAST = 2
+LAST = 3
 MESH = pl.DeviceIdType.MESH
 
 
@@ -52,10 +52,10 @@
 
 
 def step_kernel(
-    scalar_ref, tables_hbm, psi_hbm, density_in_hbm, dens_hbm, resid_hbm,
+    occ_hbm, weight_hbm, tables_hbm, psi_hbm, density_in_hbm, dens_hbm, resid_hbm,
     first_ref, others_ref, update_ref,
     tables, psi, send, recv, pools, resid, dens, density_in, share, wbuf, grams, lates,
-    late_acc, inverse,
+    late_acc, inverse, occ_ref, weight_ref,
     in_sem, psi_sem, send_sem, recv_sem, small_send, small_recv, pool_send, pool_recv,
 ):
     points, devices = lax.axis_size("ka"), lax.axis_size("band")
@@ -67,6 +67,21 @@
     flat = ka * devices + me
     half = devices // 2
     steps = [s for low in range(half - 1, -1, -1) for s in (half + low, low) if s]
+    nearby = [partner(me, s, devices) for s in range(half - 1, 0, -1)]
+    if devices % 4:
+        far = [partner(me, s, devices) for s in range(devices - 1, half - 1, -1)]
+    else:
+        quarter = devices // 4
+        side, within = me // half, lax.rem(me, quarter)
+        far = [
+            ((1 - side) * k + side * (3 - k)) * quarter + partner(within, s, quarter)
+            for k in (3, 2) for s in range(quarter)
+        ]
+    outer = [other for pair in zip(far, nearby) for other in pair] + far[len(nearby) :]
+    others = [
+        (lax.rem(ka + k, points), partner(me, s, devices))
+        for s in range(devices - 1, -1, -1) for k in range(points - 1, -1, -1) if s or k
+    ]
     some_band = (ka, partner(me, 1, devices))
     some_point = (lax.rem(ka + 1, points), me)
 
@@ -86,24 +101,21 @@
 
     psi_copy(0, 0).start()
     tables_copy.start()
+    pltpu.make_async_copy(occ_hbm, occ_ref, in_sem.at[4]).start()
+    pltpu.make_async_copy(weight_hbm, weight_ref, in_sem.at[5]).start()
     psi_copy(1, 1).start()
     barrier = pltpu.get_barrier_semaphore()
 
-    def greet(step, carry):
-        other = lax.rem(flat + step, everyone)
-        pl.semaphore_signal(
-            barrier, inc=1, device_id=(other // devices, lax.rem(other, devices)),
-            device_id_type=MESH,
-        )
-        return carry
-
-    lax.fori_loop(1, everyone, greet, 0)
+    for device in others:
+        pl.semaphore_signal(barrier, inc=1, device_id=device, device_id_type=MESH)
     base_copy.start()
     resid_copy.start()
     dens_copy.start()
     pools[pl.ds(ka, 1)] = jnp.zeros((1, depth, size, size), jnp.float32)
     late_acc[...] = jnp.zeros(late_acc.shape, jnp.float32)
-    wbuf[pl.ds(ka, 1)] = jnp.full((1, 1, 128), scalar_ref[0, bands])
+    pltpu.make_async_copy(occ_hbm, occ_ref, in_sem.at[4]).wait()
+    pltpu.make_async_copy(weight_hbm, weight_ref, in_sem.at[5]).wait()
+    wbuf[pl.ds(ka, 1)] = jnp.full((1, 1, size), weight_ref[0].astype(jnp.float32))
     tables_copy.wait()
 
     def send_planes(cut):
@@ -133,17 +145,17 @@
 
         recv[band, pl.ds(me, 1)] = send[band, pl.ds(me, 1)]
 
-    def transform(band, layers):
+    def transform(pieces):
         columns = []
-        for z in layers:
+        for band, z in pieces:
             parts = [recv[band, :, z, c].reshape(devices * planes, size) for c in range(2)]
             columns.append(jnp.concatenate(parts, axis=0))
         field = dot3(
             (tables[2], tables[3]), split(jnp.concatenate(columns, axis=1)), ((1,), (0,))
         )
         power = field[:size] * field[:size] + field[size:] * field[size:]
-        scale = share[...] * scalar_ref[0, band]
-        for i, z in enumerate(layers):
+        for i, (band, z) in enumerate(pieces):
+            scale = share[...] * occ_ref[0, band].astype(jnp.float32)
             pools[ka, z] += scale * power[:, i * size : (i + 1) * size]
 
     def consume(band):
@@ -153,7 +165,7 @@
         ).wait_recv()
 
         def body(pair, carry):
-            transform(band, (2 * pair, 2 * pair + 1))
+            transform([(band, 2 * pair), (band, 2 * pair + 1)])
             return carry
 
         lax.fori_loop(0, pairs, body, 0)
@@ -241,7 +253,12 @@
             right = jnp.where(
                 level == j, solved, jnp.where(level > j, right - column * solved, right)
             )
-        inverse[0:hist] = right
+        squared = jnp.zeros((hist, 128), jnp.float32)
+        for j in range(hist):
+            line = jnp.sum(jnp.where(level == j, right, 0.0), axis=0, keepdims=True)
+            column = jnp.sum(jnp.where(lane == level, line, 0.0), axis=1, keepdims=True)
+            squared = squared + column * line
+        inverse[0:hist] = squared
         inverse[hist : hist + 1] = start
 
     def step(band, carry):
@@ -265,8 +282,7 @@
         @pl.when(band == bands - 1)
         def _():
             def layer(z, carry):
-                for s in steps:
-                    other = partner(me, s, devices)
+                for other in outer:
                     tail = pl.ds(early, LAST)
                     remote(
                         send.at[tail, other, z], recv.at[tail, me, z],
@@ -324,8 +340,7 @@
 
     def finish(z):
         last_bands(z).wait_recv()
-        for band in range(early, bands):
-            transform(band, (z,))
+        transform([(band, z) for band in range(early, bands)])
 
     def project(z):
         for h in range(hist):
@@ -352,15 +367,10 @@
     row = jnp.sum(jnp.where(lane == level, sums, 0.0), axis=0, keepdims=True)
     lates[pl.ds(flat, 1)] = row[None]
 
-    def tell(step, carry):
-        other = lax.rem(flat + step, everyone)
+    for device in others:
         remote(
-            lates.at[flat], lates.at[flat], small_send.at[2], small_recv.at[2],
-            (other // devices, lax.rem(other, devices)),
+            lates.at[flat], lates.at[flat], small_send.at[2], small_recv.at[2], device
         ).start()
-        return carry
-
-    lax.fori_loop(1, everyone, tell, 0)
     send_pool(depth - 1)
     if depth > 1:
         gather(depth - 2)
@@ -370,14 +380,8 @@
     late = lates[0]
     for d in range(1, everyone):
         late = late + lates[d]
-    factor_inverse = inverse[0:hist]
-    halfway = jnp.sum(
-        factor_inverse * (late - inverse[hist : hist + 1]), axis=1, keepdims=True
-    )
-    coefs = jnp.sum(factor_inverse * halfway, axis=0, keepdims=True)
-    coefs = [
-        jnp.sum(jnp.where(lane[:1] == h, coefs, 0.0), axis=1, keepdims=True) for h in range(hist)
-    ]
+    coefs = jnp.sum(inverse[0:hist] * (late - inverse[hist : hist + 1]), axis=1, keepdims=True)
+    coefs = [coefs[h : h + 1] for h in range(hist)]
     for z in range(depth):
         update = coefs[0] * dens[0, z]
         for h in range(1, hist):
@@ -410,14 +414,13 @@
     tables = jnp.asarray(rotation_tables(size))
     anywhere = pl.BlockSpec(memory_space=pltpu.HBM)
     scalars = pl.BlockSpec(memory_space=pltpu.SMEM)
-    numbers = jnp.concatenate([occupations[0], weights]).astype(jnp.float32)[None]
     resident = pl.BlockSpec(memory_space=pltpu.VMEM)
     slab = jax.ShapeDtypeStruct((depth, size, size), jnp.float32)
     f32 = jnp.float32
     dma = pltpu.SemaphoreType.DMA
     first, others, update = pl.pallas_call(
         step_kernel,
-        in_specs=[scalars] + [anywhere] * 5,
+        in_specs=[anywhere] * 7,
         out_specs=[resident] * 3,
         out_shape=(slab, slab, slab),
         scratch_shapes=[
@@ -429,20 +432,21 @@
             pltpu.VMEM((hist, depth, size, size), f32),
             pltpu.VMEM((hist, depth, size, size), f32),
             pltpu.VMEM((depth, size, size), f32),
-            pltpu.VMEM((1, 128), f32),
-            pltpu.VMEM((points, 1, 128), f32),
+            pltpu.VMEM((1, size), f32),
+            pltpu.VMEM((points, 1, size), f32),
             pltpu.VMEM((devices, 1, 128), f32),
             pltpu.VMEM((points * devices, 1, 128), f32),
             pltpu.VMEM((hist, 8, size), f32),
             pltpu.VMEM((hist + 8, 128), f32),
-            dma((4,)), dma((2,)),
+            pltpu.SMEM((1, bands), jnp.int32), pltpu.SMEM((1,), jnp.int32),
+            dma((6,)), dma((2,)),
             dma((bands - LAST + depth,)), dma((bands - LAST + depth,)),
             dma((3,)), dma((3,)), dma((depth,)), dma((depth,)),
         ],
         compiler_params=pltpu.CompilerParams(
             collective_id=0, has_side_effects=True, vmem_limit_bytes=52 * 1024 * 1024
         ),
-    )(numbers, tables, psi_hat, density_in, dens_hist, resid_hist)
+    )(occupations, weights, tables, psi_hat, density_in, dens_hist, resid_hist)
     density = first + others
     return density, density_in + beta_mix * (density - density_in) - update
 

time: 289 us -> 287 us (level)
  no operation moved by 1% of the time
where the time goes in v3:
time: 287 us
  Pallas kernels  284 us (99%)
    pallas_call x1, Pallas kernels, shards(): pl.pallas_call(step_kernel, in_specs=[anywhere] * 7, out_specs=[resident]...  284 us

profile of v3, /device:TPU:0, one launch (start us, length us, event | category | flops | bytes accessed | tf_op | source)
XLA Modules:
  0.0 287.0 jit_solution(10732722543189339026)
XLA Ops:
  1.3 0.0 copy-start
  1.3 0.6 copy-done
  1.9 0.0 copy-start.1
  1.9 284.0 %shard_map.86 = (f32[8,128,128]{2,1,0:T(8,128)S(1)}, f32[8,128,128]{2,1,0:T(8,128)S(1)}, f32[8,128,128]{2,1,0:T(8,128)S(1)}) custom-call(s32[1,12]{1,0:T(1,128)S(1)} %copy-done, s32[1]{0:T(128)S(6)} %copy.9.weight_hbm, bf16[4,256,256]{2,1,0:T(8,128)(2,1)} %constant.4.clone.tables_hbm, f32[1,12,2,8,128,128]{5,4,3,2,1,0:T(8,128)} %psi_hbm.1, ...), custom_call_target="tpu_custom_call" | custom-call | tf_op jit(solution)/shard_map/pallas_call | solution.py:421
  285.9 0.0 copy-done.1
  285.9 1.1 add_subtract_fusion
Async XLA Ops:
  1.3 0.7 copy-start
  1.9 284.0 %copy-start.1 = (f32[8,128,128]{2,1,0:T(8,128)S(1)}, f32[8,128,128]{2,1,0:T(8,128)}, u32[]{:S(2)}) copy-start(f32[8,128,128]{2,1,0:T(8,128)} %density_in_hbm.1) | copy-start | bytes 1572868

commit v4 on v3

--- a/solution.py
+++ b/solution.py
@@ -119,8 +119,7 @@
     tables_copy.wait()
 
     def send_planes(cut):
-        for s in steps:
-            other = partner(me, s, devices)
+        for other in far + nearby:
             remote(
                 send.at[0, other, :, :, cut], recv.at[0, me, :, :, cut],
                 send_sem.at[0], recv_sem.at[0], (ka, other),
@@ -272,8 +271,7 @@
 
         @pl.when((band > 0) & (band < early))
         def _():
-            for s in steps:
-                other = partner(me, s, devices)
+            for other in outer:
                 remote(
                     send.at[band, other], recv.at[band, me],
                     send_sem.at[band], recv_sem.at[band], (ka, other),

time: 287 us -> 287 us (level)
  no operation moved by 1% of the time
where the time goes in v4:
time: 287 us
  Pallas kernels  284 us (99%)
    pallas_call x1, Pallas kernels, shards(): pl.pallas_call(step_kernel, in_specs=[anywhere] * 7, out_specs=[resident]...  284 us

profile of v4, /device:TPU:0, one launch (start us, length us, event | category | flops | bytes accessed | tf_op | source)
XLA Modules:
  0.0 286.9 jit_solution(9590422320572436502)
XLA Ops:
  1.3 0.0 copy-start
  1.3 0.6 copy-done
  1.9 0.0 copy-start.1
  1.9 283.9 %shard_map.86 = (f32[8,128,128]{2,1,0:T(8,128)S(1)}, f32[8,128,128]{2,1,0:T(8,128)S(1)}, f32[8,128,128]{2,1,0:T(8,128)S(1)}) custom-call(s32[1,12]{1,0:T(1,128)S(1)} %copy-done, s32[1]{0:T(128)S(6)} %copy.9.weight_hbm, bf16[4,256,256]{2,1,0:T(8,128)(2,1)} %constant.4.clone.tables_hbm, f32[1,12,2,8,128,128]{5,4,3,2,1,0:T(8,128)} %psi_hbm.1, ...), custom_call_target="tpu_custom_call" | custom-call | tf_op jit(solution)/shard_map/pallas_call | solution.py:419
  285.8 0.0 copy-done.1
  285.9 1.1 add_subtract_fusion
Async XLA Ops:
  1.3 0.7 copy-start
  1.9 283.9 %copy-start.1 = (f32[8,128,128]{2,1,0:T(8,128)S(1)}, f32[8,128,128]{2,1,0:T(8,128)}, u32[]{:S(2)}) copy-start(f32[8,128,128]{2,1,0:T(8,128)} %density_in_hbm.1) | copy-start | bytes 1572868
